TPU v7x, 32 devices: a whole 2x2x4 slice. The times are simulated.
32 devices in a mesh: fsdp: 8 (over z, x), tp: 4 (over y, core).
Axes of the slice: x: 2, y: 2, z: 4, core: 2. Of those that a mesh axis runs over, the one named last changes fastest.
Arguments:
- weight_query: bfloat16 [12288, 12288], P('fsdp', 'tp'), may hold values from -0.078125 to 0.078125
- low_query: bfloat16 [12288, 64], P('fsdp'), may hold values from -0.0546875 to 0.0546875
- high_query: bfloat16 [64, 12288], P(None, 'tp'), may hold values from -0.75 to 0.75
- weight_key: bfloat16 [12288, 12288], P('fsdp', 'tp'), may hold values from -0.078125 to 0.078125
- low_key: bfloat16 [12288, 64], P('fsdp'), may hold values from -0.0546875 to 0.0546875
- high_key: bfloat16 [64, 12288], P(None, 'tp'), may hold values from -0.75 to 0.75
- weight_value: bfloat16 [12288, 12288], P('fsdp', 'tp'), may hold values from -0.078125 to 0.078125
- low_value: bfloat16 [12288, 64], P('fsdp'), may hold values from -0.0546875 to 0.0546875
- high_value: bfloat16 [64, 12288], P(None, 'tp'), may hold values from -0.75 to 0.75
- norm_train: float32 [12288], P(('fsdp', 'tp')), may hold values from 0.25 to 1.75
- norm_step: float32 [12288], P(('fsdp', 'tp')), may hold values from -0.3 to 0.3
Outputs:
- ready_query: bfloat16 [12288, 12288], P(None, ('tp', 'fsdp'))
- ready_key: bfloat16 [12288, 12288], P(None, ('tp', 'fsdp'))
- ready_value: bfloat16 [12288, 12288], P(None, ('tp', 'fsdp'))
- factor_query: float32 [12288], P(('tp', 'fsdp'))
- factor_key: float32 [12288], P(('tp', 'fsdp'))
- factor_value: float32 [12288], P(('tp', 'fsdp'))
- serve_norm: bfloat16 [12288], replicated
All inputs are finite; a program needn't handle non-finite values. Where the computation divides by a largest or mean magnitude, that divisor is 1e-20 or more.
Results may differ from a plain program's by a relative error of at most 0.001.
Values may be sent and summed in bfloat16 or wider, within the bound.
A program may use at most 192 MiB of HBM per device.

v0:
```python
import functools

import jax
import jax.numpy as jnp
from jax import lax
from jax.experimental import pallas as pl
from jax.experimental.pallas import tpu as pltpu
from jax.sharding import PartitionSpec as P

MESH = pl.DeviceIdType.MESH
LANES = 128


def merge_kernel(
    F,
    T,
    lows_t,
    highs,
    weights,
    norm_own,
    outs,
    factor_out,
    norm_out,
    low_s,
    wbuf,
    sbuf,
    mx,
    load_sem,
    send_sem,
    recv_sem,
    mx_send,
    mx_recv,
    n_send,
    n_recv,
):
    rows = weights[0].shape[0]
    C = outs[0].shape[1]
    subs = C // LANES
    S = len(weights) * subs
    H = F // 2
    R = 768 if rows % 768 == 0 else rows
    me = lax.axis_index("fsdp")
    tp = lax.axis_index("tp")
    half, place = me // H, me % H
    f32 = jnp.float32

    def near(j):
        return half * H + (place + 1 + j) % H

    def cross(j):
        return (1 - half) * H + (place + j) % H

    def peer(j):
        return (me + 1 + j) % F

    def other(j):
        return (tp + 1 + j) % T

    barrier = pltpu.get_barrier_semaphore()

    @pl.loop(0, F - 1)
    def _(j):
        pl.semaphore_signal(barrier, inc=1, device_id={"fsdp": peer(j)}, device_id_type=MESH)

    @pl.loop(0, T - 1)
    def _(j):
        pl.semaphore_signal(barrier, inc=1, device_id={"tp": other(j)}, device_id_type=MESH)

    def columns(s, t):
        return pl.ds(pl.multiple_of(t * C + (s % subs) * LANES, LANES), LANES)

    def load(s, slot, t):
        return pltpu.make_async_copy(
            weights[s // subs].at[:, columns(s, t)], wbuf.at[slot, t], load_sem.at[slot, t]
        )

    def start_loads(s, slot):
        @pl.loop(0, F)
        def _(t):
            load(s, slot, t).start()

    def merged(s, slot, t, r):
        part = pl.ds(pl.multiple_of(r * R, R), R)
        product = jnp.dot(
            low_s[s // subs, part, :],
            highs[s // subs][:, columns(s, t)],
            preferred_element_type=f32,
        )
        return wbuf[slot, t, part, :].astype(f32) + product

    def find_maxima(s, slot):
        @pl.loop(0, F)
        def _(t):
            load(s, slot, t).wait()

            def step(r, most):
                size = jnp.abs(merged(s, slot, t, r))
                return jnp.maximum(most, jnp.max(size.reshape(R // 8, 8, LANES), axis=0))

            most = lax.fori_loop(0, rows // R, step, jnp.zeros((8, LANES), f32))
            mx[s, me, pl.ds(t, 1), :] = jnp.max(most, axis=0, keepdims=True)

    def maxima_copy(group, t, source):
        first, count = groups[group]
        return pltpu.make_async_remote_copy(
            src_ref=mx.at[pl.ds(first, count), me],
            dst_ref=mx.at[pl.ds(first, count), source],
            send_sem=mx_send.at[group, t],
            recv_sem=mx_recv.at[group, source],
            device_id={"fsdp": t},
            device_id_type=MESH,
        )

    groups = [(0, 1), (1, 1), (2, 1), (3, S - 3)]

    def send_maxima(group):
        @pl.loop(0, F - 1)
        def _(j):
            maxima_copy(group, peer(j), me).start()

    def wait_maxima(group):
        @pl.loop(0, F - 1)
        def _(j):
            maxima_copy(group, peer(j), peer(j)).wait_recv()

    def factor(s, t):
        most = mx[s, 0, pl.ds(t, 1), :]
        for source in range(1, F):
            most = jnp.maximum(most, mx[s, source, pl.ds(t, 1), :])
        return most

    def data_copy(s, t, source):
        lanes = pl.ds((s % subs) * LANES, LANES)
        return pltpu.make_async_remote_copy(
            src_ref=sbuf.at[s % 2, t],
            dst_ref=outs[s // subs].at[pl.ds(pl.multiple_of(source * rows, rows), rows), lanes],
            send_sem=send_sem.at[s % 2, t],
            recv_sem=recv_sem.at[s, source],
            device_id={"fsdp": t},
            device_id_type=MESH,
        )

    def own_copy(s):
        lanes = pl.ds((s % subs) * LANES, LANES)
        return pltpu.make_async_copy(
            sbuf.at[s % 2, me],
            outs[s // subs].at[pl.ds(pl.multiple_of(me * rows, rows), rows), lanes],
            send_sem.at[s % 2, me],
        )

    def scaled(s, slot, t, put):
        load(s, slot, t).wait()
        inverse = 1.0 / factor(s, t)

        @pl.loop(0, rows // R)
        def _(r):
            put(r, (merged(s, slot, t, r) * inverse).astype(jnp.bfloat16))

    def send_block(s, slot, t):
        if s >= 2:
            data_copy(s - 2, t, me).wait_send()

        def put(r, value):
            sbuf[s % 2, t, pl.ds(pl.multiple_of(r * R, R), R), :] = value

        scaled(s, slot, t, put)
        data_copy(s, t, me).start()

    def send_stage(s, slot):
        for count, target in [(H, cross), (H - 1, near)][:: 1 if s == 0 else -1]:

            @pl.loop(0, count)
            def _(j):
                send_block(s, slot, target(j))

        if s >= 2:
            own_copy(s - 2).wait()

        def put(r, value):
            sbuf[s % 2, me, pl.ds(pl.multiple_of(r * R, R), R), :] = value

        scaled(s, slot, me, put)
        own_copy(s).start()
        factor_out[s] = factor(s, me)

    visits = [(1, 0), (1, 1), (2, 0), (1, 2), (2, 1)]
    visits += [(1, s) for s in range(3, S)] + [(2, s) for s in range(2, S)]

    start_loads(0, 0)
    greeted = False
    for v, (kind, s) in enumerate(visits):
        slot = v % 2
        if v + 1 < len(visits):
            start_loads(visits[v + 1][1], 1 - slot)
        if kind == 1:
            if s % subs == 0:
                m = s // subs
                low_s[m] = (lows_t[m][...].astype(f32) * 2.0).T.astype(jnp.bfloat16)
            find_maxima(s, slot)
            if not greeted:
                greeted = True
                pl.semaphore_wait(barrier, F + T - 2)
            if s < 3:
                send_maxima(s)
            elif s == S - 1:
                send_maxima(3)
        else:
            if s < 4:
                wait_maxima(s)
            send_stage(s, slot)
        if v == 3:
            norm_out[me, tp] = norm_own[...]

            def norm_copy(t, source):
                return pltpu.make_async_remote_copy(
                    src_ref=norm_own,
                    dst_ref=norm_out.at[source, tp],
                    send_sem=n_send.at[t],
                    recv_sem=n_recv.at[source],
                    device_id={"fsdp": t},
                    device_id_type=MESH,
                )

            @pl.loop(0, F - 1)
            def _(j):
                norm_copy(peer(j), me).start()

    @pl.loop(0, F - 1)
    def _(j):
        norm_copy(peer(j), peer(j)).wait()

    def share(t, source):
        return pltpu.make_async_remote_copy(
            src_ref=norm_out.at[:, tp],
            dst_ref=norm_out.at[:, source],
            send_sem=n_send.at[F + t],
            recv_sem=n_recv.at[F + source],
            device_id={"tp": t},
            device_id_type=MESH,
        )

    @pl.loop(0, T - 1)
    def _(j):
        share(other(j), tp).start()

    @pl.loop(0, T - 1)
    def _(j):
        share(other(j), other(j)).wait()

    for group in range(4):

        @pl.loop(0, F - 1)
        def _(j):
            maxima_copy(group, peer(j), me).wait_send()

    for s in range(S):
        if s >= S - 2:
            own_copy(s).wait()

        @pl.loop(0, F - 1)
        def _(j):
            if s >= S - 2:
                data_copy(s, peer(j), me).wait_send()
            data_copy(s, peer(j), peer(j)).wait_recv()


def entry(F, T, *refs):
    lows_t, highs, weights = refs[0:3], refs[3:6], refs[6:9]
    merge_kernel(F, T, lows_t, highs, weights, refs[9], refs[10:13], *refs[13:])


def fused(F, T, wq, lq, hq, wk, lk, hk, wv, lv, hv, norm_train, norm_step):
    rows, width = wq.shape
    rank = lq.shape[1]
    C = width // F
    S = 3 * (C // LANES)
    N = norm_train.shape[0]
    f32, bf16 = jnp.float32, jnp.bfloat16
    vmem = pl.BlockSpec(memory_space=pltpu.VMEM)
    hbm = pl.BlockSpec(memory_space=pl.ANY)
    *ready, factors, norm = pl.pallas_call(
        functools.partial(entry, F, T),
        out_shape=[jax.ShapeDtypeStruct((F * rows, C), bf16)] * 3
        + [jax.ShapeDtypeStruct((S, 1, LANES), f32), jax.ShapeDtypeStruct((F, T, 1, N), f32)],
        in_specs=[vmem] * 6 + [hbm] * 3 + [vmem],
        out_specs=[pl.BlockSpec(memory_space=pl.ANY)] * 3 + [vmem] * 2,
        scratch_shapes=[
            pltpu.VMEM((3, rows, rank), bf16),
            pltpu.VMEM((2, F, rows, LANES), bf16),
            pltpu.VMEM((2, F, rows, LANES), bf16),
            pltpu.VMEM((S, F, F, LANES), f32),
            pltpu.SemaphoreType.DMA((2, F)),
            pltpu.SemaphoreType.DMA((2, F)),
            pltpu.SemaphoreType.DMA((S, F)),
            pltpu.SemaphoreType.DMA((4, F)),
            pltpu.SemaphoreType.DMA((4, F)),
            pltpu.SemaphoreType.DMA((F + T,)),
            pltpu.SemaphoreType.DMA((F + T,)),
        ],
        compiler_params=pltpu.CompilerParams(
            collective_id=0, has_side_effects=True, vmem_limit_bytes=60000000
        ),
    )(lq.T, lk.T, lv.T, hq, hk, hv, wq, wk, wv, (norm_train + norm_step)[None])
    factors = factors.reshape(3, C)
    return (*ready, factors[0], factors[1], factors[2], norm.reshape(F * T * N).astype(bf16))


mix_rate = 2.0


def local(
    weight_query,
    low_query,
    high_query,
    weight_key,
    low_key,
    high_key,
    weight_value,
    low_value,
    high_value,
    norm_train,
    norm_step,
):
    latest_query = weight_query.astype(jnp.float32) + mix_rate * jnp.dot(
        low_query, high_query, preferred_element_type=jnp.float32
    )
    latest_key = weight_key.astype(jnp.float32) + mix_rate * jnp.dot(
        low_key, high_key, preferred_element_type=jnp.float32
    )
    latest_value = weight_value.astype(jnp.float32) + mix_rate * jnp.dot(
        low_value, high_value, preferred_element_type=jnp.float32
    )
    factor_query, factor_key, factor_value = lax.pmax(
        (
            jnp.max(jnp.abs(latest_query), axis=0),
            jnp.max(jnp.abs(latest_key), axis=0),
            jnp.max(jnp.abs(latest_value), axis=0),
        ),
        "fsdp",
    )
    narrow_query, narrow_key, narrow_value = (
        (latest_query / factor_query).astype(jnp.bfloat16),
        (latest_key / factor_key).astype(jnp.bfloat16),
        (latest_value / factor_value).astype(jnp.bfloat16),
    )
    ready_query, ready_key, ready_value = (
        lax.all_to_all(narrow_query, "fsdp", split_axis=1, concat_axis=0, tiled=True),
        lax.all_to_all(narrow_key, "fsdp", split_axis=1, concat_axis=0, tiled=True),
        lax.all_to_all(narrow_value, "fsdp", split_axis=1, concat_axis=0, tiled=True),
    )
    place = lax.axis_index("fsdp")
    factor_query = lax.dynamic_slice_in_dim(
        factor_query, place * ready_query.shape[1], ready_query.shape[1]
    )
    factor_key = lax.dynamic_slice_in_dim(
        factor_key, place * ready_key.shape[1], ready_key.shape[1]
    )
    factor_value = lax.dynamic_slice_in_dim(
        factor_value, place * ready_value.shape[1], ready_value.shape[1]
    )
    serve_norm = lax.all_gather(
        (norm_train + norm_step).astype(jnp.bfloat16), ("fsdp", "tp"), axis=0, tiled=True
    )
    return (ready_query, ready_key, ready_value, factor_query, factor_key, factor_value, serve_norm)


def solution(mesh):
    F, T = mesh.shape["fsdp"], mesh.shape["tp"]

    def step(*args):
        rows, width = args[0].shape
        if width % (F * LANES) or width < 2 * F * LANES or rows % 16 or F % 2 or T < 2:
            return local(*args)
        return fused(F, T, *args)

    return jax.shard_map(
        step,
        mesh=mesh,
        in_specs=(
            P("fsdp", "tp"),
            P("fsdp", None),
            P(None, "tp"),
            P("fsdp", "tp"),
            P("fsdp", None),
            P(None, "tp"),
            P("fsdp", "tp"),
            P("fsdp", None),
            P(None, "tp"),
            P(("fsdp", "tp")),
            P(("fsdp", "tp")),
        ),
        out_specs=(
            P(None, ("tp", "fsdp")),
            P(None, ("tp", "fsdp")),
            P(None, ("tp", "fsdp")),
            P(("tp", "fsdp")),
            P(("tp", "fsdp")),
            P(("tp", "fsdp")),
            P(),
        ),
        check_vma=False,
    )
```

profile of v0, /device:TPU:14, one launch (start us, length us, event | category | flops | bytes accessed | tf_op | source)
XLA Modules:
  0.0 670.0 jit_solution(2021380507168465346)
XLA Ops:
  0.6 0.7 add.3
  1.3 0.6 broadcast_in_dim.3.refs_9_
  1.9 646.6 %shard_map.162 = (bf16[12288,384]{1,0:T(8,128)(2,1)}, bf16[12288,384]{1,0:T(8,128)(2,1)}, bf16[12288,384]{1,0:T(8,128)(2,1)}, f32[9,1,128]{2,1,0:T(1,128)}, f32[8,4,1,384]{3,2,1,0:T(1,128)}) custom-call(bf16[64,1536]{1,0:T(8,128)(2,1)} %bitcast.8, bf16[64,1536]{1,0:T(8,128)(2,1)} %bitcast.9, bf16[64,1536]{1,0:T(8,128)(2,1)} %bitcast.10, ...), custom_call_target="tpu_custom_call" | custom-call | tf_op jit(solution)/shard_map/pallas_call | solution.py:281
  648.5 1.3 slice_reduce_fusion
  649.8 0.9 convert_reduce_fusion
  650.7 0.6 convert_element_type.7
  651.4 0.0 copy-start
  651.4 0.0 slice-start
  651.4 0.0 slice-start.1
  651.4 11.0 %copy.21 = bf16[12288,384]{1,0:T(8,128)(2,1)} copy(bf16[12288,384]{1,0:T(8,128)(2,1)} %get-tuple-element.27) | data formatting | bytes 18874368
  662.4 0.0 copy-done
  662.4 0.0 slice-start.2
  662.4 3.8 copy.22
  666.2 0.0 slice-done
  666.2 0.0 slice-done.1
  666.2 0.0 slice-done.2
  666.2 3.7 copy.23
  (1 shorter events, 0.0 us)
Async XLA Ops:
  651.4 11.0 %copy-start = (bf16[12288,384]{1,0:T(8,128)(2,1)S(1)}, bf16[12288,384]{1,0:T(8,128)(2,1)}, u32[]{:S(2)}) copy-start(bf16[12288,384]{1,0:T(8,128)(2,1)} %get-tuple-element.28) | copy-start | bytes 28311556
  651.4 14.9 %slice-start = ((s8[9437184]{0:T(1024)(128)(4,1)}), s8[4194304]{0:T(1024)(128)(4,1)S(1)}, s32[]{:S(2)}) async-start(s8[9437184]{0:T(1024)(128)(4,1)} %bitcast.6), calls=%async_computation | async-start | bytes 8388608
  651.4 14.9 %slice-start.1 = ((s8[9437184]{0:T(1024)(128)(4,1)}), s8[4194304]{0:T(1024)(128)(4,1)S(1)}, s32[]{:S(2)}) async-start(s8[9437184]{0:T(1024)(128)(4,1)} %bitcast.6), calls=%async_computation.1 | async-start | bytes 8388608
  662.4 3.9 slice-start.2
where the time goes:
time: 670 us
  Pallas kernels  647 us (97%)
  local copies, waits for them, and re-layouts  21.1 us (3%)
    pallas_call x1, Pallas kernels, fused(): pl.pallas_call(functools.partial(entry, F, T), out_shape=[jax.ShapeDtypeS...  647 us
    unnamed x11, local copies, waits for them, and re-layouts  18.6 us

commit v1 on v0

--- a/solution.py
+++ b/solution.py
@@ -17,14 +17,19 @@
     lows_t,
     highs,
     weights,
-    norm_own,
+    norms,
     outs,
     factor_out,
     norm_out,
+    low_t,
+    high,
     low_s,
+    norm_in,
     wbuf,
     sbuf,
     mx,
+    in_sem,
+    norm_sem,
     load_sem,
     send_sem,
     recv_sem,
@@ -35,20 +40,24 @@
 ):
     rows = weights[0].shape[0]
     C = outs[0].shape[1]
+    K = norm_in.shape[1] // LANES
     subs = C // LANES
     S = len(weights) * subs
     H = F // 2
+    G = H // 2
     R = 768 if rows % 768 == 0 else rows
     me = lax.axis_index("fsdp")
     tp = lax.axis_index("tp")
     half, place = me // H, me % H
+    z, x = place // 2, place % 2
+    turn = z + tp % 2
     f32 = jnp.float32
 
+    def cross(j):
+        return (1 - half) * H + (j + turn) % G * 2 + (j // G + x + turn) % 2
+
     def near(j):
-        return half * H + (place + 1 + j) % H
-
-    def cross(j):
-        return (1 - half) * H + (place + j) % H
+        return half * H + (j + 1 + z) % G * 2 + ((j + 1) // G + x) % 2
 
     def peer(j):
         return (me + 1 + j) % F
@@ -79,11 +88,20 @@
         def _(t):
             load(s, slot, t).start()
 
+    def inputs(m):
+        return (
+            pltpu.make_async_copy(lows_t[m], low_t.at[m], in_sem.at[m, 0]),
+            pltpu.make_async_copy(highs[m], high.at[m], in_sem.at[m, 1]),
+        )
+
+    def norm_inputs():
+        return [pltpu.make_async_copy(norms[i], norm_in.at[i], norm_sem.at[i]) for i in range(2)]
+
     def merged(s, slot, t, r):
         part = pl.ds(pl.multiple_of(r * R, R), R)
         product = jnp.dot(
             low_s[s // subs, part, :],
-            highs[s // subs][:, columns(s, t)],
+            high[s // subs, :, columns(s, t)],
             preferred_element_type=f32,
         )
         return wbuf[slot, t, part, :].astype(f32) + product
@@ -140,14 +158,6 @@
             device_id_type=MESH,
         )
 
-    def own_copy(s):
-        lanes = pl.ds((s % subs) * LANES, LANES)
-        return pltpu.make_async_copy(
-            sbuf.at[s % 2, me],
-            outs[s // subs].at[pl.ds(pl.multiple_of(me * rows, rows), rows), lanes],
-            send_sem.at[s % 2, me],
-        )
-
     def scaled(s, slot, t, put):
         load(s, slot, t).wait()
         inverse = 1.0 / factor(s, t)
@@ -167,26 +177,43 @@
         data_copy(s, t, me).start()
 
     def send_stage(s, slot):
-        for count, target in [(H, cross), (H - 1, near)][:: 1 if s == 0 else -1]:
-
-            @pl.loop(0, count)
-            def _(j):
-                send_block(s, slot, target(j))
-
-        if s >= 2:
-            own_copy(s - 2).wait()
+        @pl.loop(0, H - 1)
+        def _(j):
+            send_block(s, slot, cross(j))
+            send_block(s, slot, near(j))
+
+        send_block(s, slot, cross(H - 1))
 
         def put(r, value):
-            sbuf[s % 2, me, pl.ds(pl.multiple_of(r * R, R), R), :] = value
+            lanes = pl.ds((s % subs) * LANES, LANES)
+            outs[s // subs][pl.ds(pl.multiple_of(me * rows + r * R, R), R), lanes] = value
 
         scaled(s, slot, me, put)
-        own_copy(s).start()
         factor_out[s] = factor(s, me)
 
     visits = [(1, 0), (1, 1), (2, 0), (1, 2), (2, 1)]
     visits += [(1, s) for s in range(3, S)] + [(2, s) for s in range(2, S)]
 
+    for copy in inputs(0):
+        copy.start()
     start_loads(0, 0)
+    for m in range(1, len(weights)):
+        for copy in inputs(m):
+            copy.start()
+    for copy in norm_inputs():
+        copy.start()
+
+    def norm_copy(t, source):
+        mine = norm_out.at[source, pl.ds(tp * K, K)]
+        return pltpu.make_async_remote_copy(
+            src_ref=norm_out.at[me, pl.ds(tp * K, K)],
+            dst_ref=mine,
+            send_sem=n_send.at[t],
+            recv_sem=n_recv.at[source],
+            device_id={"fsdp": t},
+            device_id_type=MESH,
+        )
+
     greeted = False
     for v, (kind, s) in enumerate(visits):
         slot = v % 2
@@ -195,7 +222,9 @@
         if kind == 1:
             if s % subs == 0:
                 m = s // subs
-                low_s[m] = (lows_t[m][...].astype(f32) * 2.0).T.astype(jnp.bfloat16)
+                for copy in inputs(m):
+                    copy.wait()
+                low_s[m] = (low_t[m].astype(f32) * 2.0).T.astype(jnp.bfloat16)
             find_maxima(s, slot)
             if not greeted:
                 greeted = True
@@ -209,17 +238,11 @@
                 wait_maxima(s)
             send_stage(s, slot)
         if v == 3:
-            norm_out[me, tp] = norm_own[...]
-
-            def norm_copy(t, source):
-                return pltpu.make_async_remote_copy(
-                    src_ref=norm_own,
-                    dst_ref=norm_out.at[source, tp],
-                    send_sem=n_send.at[t],
-                    recv_sem=n_recv.at[source],
-                    device_id={"fsdp": t},
-                    device_id_type=MESH,
-                )
+            for copy in norm_inputs():
+                copy.wait()
+            for k in range(K):
+                part = pl.ds(k * LANES, LANES)
+                norm_out[me, tp * K + k] = norm_in[0:1, part] + norm_in[1:2, part]
 
             @pl.loop(0, F - 1)
             def _(j):
@@ -231,8 +254,8 @@
 
     def share(t, source):
         return pltpu.make_async_remote_copy(
-            src_ref=norm_out.at[:, tp],
-            dst_ref=norm_out.at[:, source],
+            src_ref=norm_out.at[:, pl.ds(tp * K, K)],
+            dst_ref=norm_out.at[:, pl.ds(source * K, K)],
             send_sem=n_send.at[F + t],
             recv_sem=n_recv.at[F + source],
             device_id={"tp": t},
@@ -254,8 +277,6 @@
             maxima_copy(group, peer(j), me).wait_send()
 
     for s in range(S):
-        if s >= S - 2:
-            own_copy(s).wait()
 
         @pl.loop(0, F - 1)
         def _(j):
@@ -265,30 +286,57 @@
 
 
 def entry(F, T, *refs):
-    lows_t, highs, weights = refs[0:3], refs[3:6], refs[6:9]
-    merge_kernel(F, T, lows_t, highs, weights, refs[9], refs[10:13], *refs[13:])
+    lows_t, highs, weights, norms = refs[0:3], refs[3:6], refs[6:9], refs[9:11]
+    merge_kernel(F, T, lows_t, highs, weights, norms, refs[11:14], *refs[14:])
+
+
+def finish_kernel(*refs):
+    ready, (factors, norm), ready_out, factor_out = refs[0:3], refs[3:5], refs[5:8], refs[8:11]
+    norm_out, factor_buf, norm_buf, ready_sem, small_sem = refs[11:]
+    copies = [
+        pltpu.make_async_copy(ready[m], ready_out[m], ready_sem.at[m]) for m in range(3)
+    ]
+    subs = factors.shape[0] // 3
+    for copy in copies:
+        copy.start()
+    for m in range(3):
+        factor_buf[m] = factors[m * subs : (m + 1) * subs, 0, :]
+        copies.append(pltpu.make_async_copy(factor_buf.at[m], factor_out[m], small_sem.at[m]))
+        copies[-1].start()
+    norm_buf[...] = norm[:, 0, :].astype(norm_buf.dtype)
+    copies.append(pltpu.make_async_copy(norm_buf, norm_out, small_sem.at[3]))
+    copies[-1].start()
+    for copy in copies:
+        copy.wait()
 
 
 def fused(F, T, wq, lq, hq, wk, lk, hk, wv, lv, hv, norm_train, norm_step):
     rows, width = wq.shape
     rank = lq.shape[1]
     C = width // F
-    S = 3 * (C // LANES)
+    subs = C // LANES
+    S = 3 * subs
     N = norm_train.shape[0]
+    K = N // LANES
     f32, bf16 = jnp.float32, jnp.bfloat16
+    hbm = pl.BlockSpec(memory_space=pl.ANY)
     vmem = pl.BlockSpec(memory_space=pltpu.VMEM)
-    hbm = pl.BlockSpec(memory_space=pl.ANY)
     *ready, factors, norm = pl.pallas_call(
         functools.partial(entry, F, T),
-        out_shape=[jax.ShapeDtypeStruct((F * rows, C), bf16)] * 3
-        + [jax.ShapeDtypeStruct((S, 1, LANES), f32), jax.ShapeDtypeStruct((F, T, 1, N), f32)],
-        in_specs=[vmem] * 6 + [hbm] * 3 + [vmem],
-        out_specs=[pl.BlockSpec(memory_space=pl.ANY)] * 3 + [vmem] * 2,
+        out_shape=[pltpu.VMEM((F * rows, C), bf16)] * 3
+        + [pltpu.VMEM((S, 1, LANES), f32), pltpu.VMEM((F, T * K, 1, LANES), f32)],
+        in_specs=[hbm] * 11,
+        out_specs=[vmem] * 5,
         scratch_shapes=[
+            pltpu.VMEM((3, rank, rows), bf16),
+            pltpu.VMEM((3, rank, width), bf16),
             pltpu.VMEM((3, rows, rank), bf16),
+            pltpu.VMEM((2, N), f32),
             pltpu.VMEM((2, F, rows, LANES), bf16),
             pltpu.VMEM((2, F, rows, LANES), bf16),
             pltpu.VMEM((S, F, F, LANES), f32),
+            pltpu.SemaphoreType.DMA((3, 2)),
+            pltpu.SemaphoreType.DMA((2,)),
             pltpu.SemaphoreType.DMA((2, F)),
             pltpu.SemaphoreType.DMA((2, F)),
             pltpu.SemaphoreType.DMA((S, F)),
@@ -298,11 +346,26 @@
             pltpu.SemaphoreType.DMA((F + T,)),
         ],
         compiler_params=pltpu.CompilerParams(
-            collective_id=0, has_side_effects=True, vmem_limit_bytes=60000000
+            collective_id=0, has_side_effects=True, vmem_limit_bytes=30000000
         ),
-    )(lq.T, lk.T, lv.T, hq, hk, hv, wq, wk, wv, (norm_train + norm_step)[None])
-    factors = factors.reshape(3, C)
-    return (*ready, factors[0], factors[1], factors[2], norm.reshape(F * T * N).astype(bf16))
+    )(lq.T, lk.T, lv.T, hq, hk, hv, wq, wk, wv, norm_train, norm_step)
+    norm = norm.reshape(F * T * K, 1, LANES)
+    results = pl.pallas_call(
+        finish_kernel,
+        out_shape=[jax.ShapeDtypeStruct((F * rows, C), bf16)] * 3
+        + [jax.ShapeDtypeStruct((subs, LANES), f32)] * 3
+        + [jax.ShapeDtypeStruct((F * T * K, LANES), bf16)],
+        in_specs=[vmem] * 5,
+        out_specs=[hbm] * 7,
+        scratch_shapes=[
+            pltpu.VMEM((3, subs, LANES), f32),
+            pltpu.VMEM((F * T * K, LANES), bf16),
+            pltpu.SemaphoreType.DMA((3,)),
+            pltpu.SemaphoreType.DMA((4,)),
+        ],
+        compiler_params=pltpu.CompilerParams(vmem_limit_bytes=2000000),
+    )(*[pltpu.with_memory_space_constraint(a, pltpu.VMEM) for a in (*ready, factors, norm)])
+    return (*results[:3], *[a.reshape(C) for a in results[3:6]], results[6].reshape(F * T * N))
 
 
 mix_rate = 2.0
@@ -369,7 +432,8 @@
 
     def step(*args):
         rows, width = args[0].shape
-        if width % (F * LANES) or width < 2 * F * LANES or rows % 16 or F % 2 or T < 2:
+        aligned = width % (F * LANES) == 0 and args[9].shape[0] % LANES == 0
+        if not aligned or width < 2 * F * LANES or rows % 16 or F % 4 or T < 2:
             return local(*args)
         return fused(F, T, *args)
 

time: 670 us -> 647 us (0.966)
  local copies, waits for them, and re-layouts: 21.1 us -> 7.42 us
  Pallas kernels: 647 us -> 636 us
    unnamed x11 -> x4, local copies, waits for them, and re-layouts: 18.6 us -> 7.42 us
    pallas_call x1 -> x2, Pallas kernels: 647 us -> 636 us  [the longest x1 626 us: fused(): pl.pallas_call(functools.partial(entry, F, T), out_shape=[pltpu.VMEM((F *...]
where the time goes in v1:
time: 647 us; the launch traced here: 644 us
  Pallas kernels  636 us (98%)
  local copies, waits for them, and re-layouts  7.42 us (1%)
    pallas_call x1, Pallas kernels, fused(): pl.pallas_call(functools.partial(entry, F, T), out_shape=[pltpu.VMEM((F *...  626 us

profile of v1, /device:TPU:14, one launch (start us, length us, event | category | flops | bytes accessed | tf_op | source)
XLA Modules:
  0.0 644.1 jit_solution(17754996663992836312)
XLA Ops:
  0.6 626.3 %shard_map.162 = (bf16[12288,384]{1,0:T(8,128)(2,1)S(1)}, bf16[12288,384]{1,0:T(8,128)(2,1)S(1)}, bf16[12288,384]{1,0:T(8,128)(2,1)S(1)}, f32[9,1,128]{2,1,0:T(1,128)S(1)}, f32[8,12,1,128]{3,2,1,0:T(1,128)S(1)}) custom-call(bf16[64,1536]{1,0:T(8,128)(2,1)} %bitcast.9, bf16[64,1536]{1,0:T(8,128)(2,1)} %bitcast.10, bf16[64,1536]{1,0:T(8,128)(2,1)} %bitcast.11, ...), custom_call_target="tpu_custom_call" | custom-call | tf_op jit(solution)/shard_map/pallas_call | solution.py:324
  626.9 0.0 copy-start
  626.9 3.7 copy-done
  630.7 0.0 copy-start.1
  630.7 3.7 copy-done.1
  634.3 9.8 %shard_map.163 = (bf16[12288,384]{1,0:T(8,128)(2,1)}, bf16[12288,384]{1,0:T(8,128)(2,1)}, bf16[12288,384]{1,0:T(8,128)(2,1)}, f32[3,128]{1,0:T(4,128)}, f32[3,12...) custom-call(bf16[12288,384]{1,0:T(8,128)(2,1)S(1)} %copy-done.1, ...), custom_call_target="tpu_custom_call" | custom-call | tf_op jit(solution)/shard_map/pallas_call | solution.py:353
Async XLA Ops:
  626.9 3.7 copy-start
  630.7 3.7 copy-start.1

commit v2 on v1

--- a/solution.py
+++ b/solution.py
@@ -9,6 +9,8 @@
 
 MESH = pl.DeviceIdType.MESH
 LANES = 128
+EARLY = 2
+AHEAD = 3
 
 
 def merge_kernel(
@@ -27,7 +29,10 @@
     norm_in,
     wbuf,
     sbuf,
-    mx,
+    first,
+    own,
+    got,
+    fac,
     in_sem,
     norm_sem,
     load_sem,
@@ -35,6 +40,9 @@
     recv_sem,
     mx_send,
     mx_recv,
+    low_in,
+    early_send,
+    early_recv,
     n_send,
     n_recv,
 ):
@@ -45,7 +53,7 @@
     S = len(weights) * subs
     H = F // 2
     G = H // 2
-    R = 768 if rows % 768 == 0 else rows
+    R = rows if rows <= 1536 else 768 if rows % 768 == 0 else rows
     me = lax.axis_index("fsdp")
     tp = lax.axis_index("tp")
     half, place = me // H, me % H
@@ -56,6 +64,10 @@
     def cross(j):
         return (1 - half) * H + (j + turn) % G * 2 + (j // G + x + turn) % 2
 
+    def source(j):
+        above = (z - j - tp % 2) % G
+        return (1 - half) * H + above * 2 + (x - j // G - above - tp % 2) % 2
+
     def near(j):
         return half * H + (j + 1 + z) % G * 2 + ((j + 1) // G + x) % 2
 
@@ -116,87 +128,162 @@
                 return jnp.maximum(most, jnp.max(size.reshape(R // 8, 8, LANES), axis=0))
 
             most = lax.fori_loop(0, rows // R, step, jnp.zeros((8, LANES), f32))
-            mx[s, me, pl.ds(t, 1), :] = jnp.max(most, axis=0, keepdims=True)
-
-    def maxima_copy(group, t, source):
-        first, count = groups[group]
+            most = jnp.max(most, axis=0, keepdims=True)
+            own[t, s : s + 1, :] = most
+            if s == 0:
+                first[me, pl.ds(t, 1), :] = most
+
+    def maxima_copy(kind, t, source):
+        pairs = [
+            (first.at[me], first.at[source]),
+            (own.at[t], got.at[source]),
+            (fac.at[me], fac.at[source]),
+        ]
         return pltpu.make_async_remote_copy(
-            src_ref=mx.at[pl.ds(first, count), me],
-            dst_ref=mx.at[pl.ds(first, count), source],
-            send_sem=mx_send.at[group, t],
-            recv_sem=mx_recv.at[group, source],
+            src_ref=pairs[kind][0],
+            dst_ref=pairs[kind][1],
+            send_sem=mx_send.at[kind, t],
+            recv_sem=mx_recv.at[kind, source],
             device_id={"fsdp": t},
             device_id_type=MESH,
         )
 
-    groups = [(0, 1), (1, 1), (2, 1), (3, S - 3)]
-
-    def send_maxima(group):
+    def send_maxima(kind):
         @pl.loop(0, F - 1)
         def _(j):
-            maxima_copy(group, peer(j), me).start()
-
-    def wait_maxima(group):
+            maxima_copy(kind, peer(j), me).start()
+
+    def wait_maxima(kind):
         @pl.loop(0, F - 1)
         def _(j):
-            maxima_copy(group, peer(j), peer(j)).wait_recv()
+            maxima_copy(kind, peer(j), peer(j)).wait_recv()
+
+    def reduce_maxima():
+        most = own[me]
+        for j in range(F - 1):
+            most = jnp.maximum(most, got[peer(j)])
+        fac[me] = most
+        for s in range(S):
+            factor_out[s] = most[s : s + 1, :]
 
     def factor(s, t):
-        most = mx[s, 0, pl.ds(t, 1), :]
+        if s > 0:
+            return fac[t, s : s + 1, :]
+        most = first[0, pl.ds(t, 1), :]
         for source in range(1, F):
-            most = jnp.maximum(most, mx[s, source, pl.ds(t, 1), :])
+            most = jnp.maximum(most, first[source, pl.ds(t, 1), :])
         return most
 
-    def data_copy(s, t, source):
+    def data_copy(s, t, source, early=False):
         lanes = pl.ds((s % subs) * LANES, LANES)
+        skip = LANES if early else 0
+        start = pl.multiple_of(source * rows + skip, LANES)
         return pltpu.make_async_remote_copy(
-            src_ref=sbuf.at[s % 2, t],
-            dst_ref=outs[s // subs].at[pl.ds(pl.multiple_of(source * rows, rows), rows), lanes],
+            src_ref=sbuf.at[s % 2, t, pl.ds(skip, rows - skip)],
+            dst_ref=outs[s // subs].at[pl.ds(start, rows - skip), lanes],
             send_sem=send_sem.at[s % 2, t],
             recv_sem=recv_sem.at[s, source],
             device_id={"fsdp": t},
             device_id_type=MESH,
         )
 
+    def on_data(s, t, source, j, act):
+        if s >= subs or j is None:
+            act(data_copy(s, t, source))
+        else:
+
+            @pl.when(j < EARLY)
+            def _():
+                act(data_copy(s, t, source, True))
+
+            @pl.when(j >= EARLY)
+            def _():
+                act(data_copy(s, t, source))
+
+    def early_copies(j, t, source):
+        piece = pl.ds(0, LANES)
+        part = pl.ds(pl.multiple_of(source * rows, LANES), LANES)
+        wide = pl.ds(pl.multiple_of(t * C, LANES), C)
+        pairs = [(weights[0].at[piece, wide], outs[0].at[part]), (lows_t[0].at[:, piece], low_in.at[j])]
+        return [
+            pltpu.make_async_remote_copy(
+                src_ref=src,
+                dst_ref=dst,
+                send_sem=early_send.at[j, i],
+                recv_sem=early_recv.at[j, i],
+                device_id={"fsdp": t},
+                device_id_type=MESH,
+            )
+            for i, (src, dst) in enumerate(pairs)
+        ]
+
+    def finish_early():
+        @pl.loop(0, EARLY)
+        def _(j):
+            for copy in early_copies(j, cross(j), me):
+                copy.wait_send()
+            for copy in early_copies(j, source(j), source(j)):
+                copy.wait_recv()
+            low = (low_in[j].astype(f32) * 2.0).T.astype(jnp.bfloat16)
+            part = pl.ds(pl.multiple_of(source(j) * rows, LANES), LANES)
+            for s in range(subs):
+                lanes = pl.ds(s * LANES, LANES)
+                product = jnp.dot(low, high[0, :, columns(s, me)], preferred_element_type=f32)
+                value = outs[0][part, lanes].astype(f32) + product
+                outs[0][part, lanes] = (value * (1.0 / factor(s, me))).astype(jnp.bfloat16)
+
     def scaled(s, slot, t, put):
-        load(s, slot, t).wait()
+        if s > 0:
+            load(s, slot, t).wait()
         inverse = 1.0 / factor(s, t)
 
         @pl.loop(0, rows // R)
         def _(r):
             put(r, (merged(s, slot, t, r) * inverse).astype(jnp.bfloat16))
 
-    def send_block(s, slot, t):
+    def send_block(s, slot, t, j=None):
         if s >= 2:
-            data_copy(s - 2, t, me).wait_send()
+            on_data(s - 2, t, me, j, lambda copy: copy.wait_send())
 
         def put(r, value):
             sbuf[s % 2, t, pl.ds(pl.multiple_of(r * R, R), R), :] = value
 
         scaled(s, slot, t, put)
-        data_copy(s, t, me).start()
-
-    def send_stage(s, slot):
-        @pl.loop(0, H - 1)
-        def _(j):
-            send_block(s, slot, cross(j))
+        on_data(s, t, me, j, lambda copy: copy.start())
+
+    def send_pairs(s, slot, begin, end):
+        @pl.loop(begin, end)
+        def _(j):
+            send_block(s, slot, cross(j), j)
             send_block(s, slot, near(j))
 
-        send_block(s, slot, cross(H - 1))
+    def send_last(s, slot):
+        send_block(s, slot, cross(H - 1), H - 1)
 
         def put(r, value):
             lanes = pl.ds((s % subs) * LANES, LANES)
             outs[s // subs][pl.ds(pl.multiple_of(me * rows + r * R, R), R), lanes] = value
 
         scaled(s, slot, me, put)
-        factor_out[s] = factor(s, me)
-
-    visits = [(1, 0), (1, 1), (2, 0), (1, 2), (2, 1)]
-    visits += [(1, s) for s in range(3, S)] + [(2, s) for s in range(2, S)]
+
+    queue = [(kind, s) for kind in (1, 2) for s in range(1, S)]
+
+    def prefetch(v):
+        if v < len(queue):
+            start_loads(queue[v][1], v % 2)
+
+    def visit_maxima(s, slot):
+        if s % subs == 0:
+            m = s // subs
+            for copy in inputs(m):
+                copy.wait()
+            low_s[m] = (low_t[m].astype(f32) * 2.0).T.astype(jnp.bfloat16)
+        find_maxima(s, slot)
 
     for copy in inputs(0):
         copy.start()
-    start_loads(0, 0)
+    start_loads(0, 2)
+    prefetch(0)
     for m in range(1, len(weights)):
         for copy in inputs(m):
             copy.start()
@@ -214,39 +301,49 @@
             device_id_type=MESH,
         )
 
-    greeted = False
-    for v, (kind, s) in enumerate(visits):
-        slot = v % 2
-        if v + 1 < len(visits):
-            start_loads(visits[v + 1][1], 1 - slot)
-        if kind == 1:
-            if s % subs == 0:
-                m = s // subs
-                for copy in inputs(m):
-                    copy.wait()
-                low_s[m] = (low_t[m].astype(f32) * 2.0).T.astype(jnp.bfloat16)
-            find_maxima(s, slot)
-            if not greeted:
-                greeted = True
-                pl.semaphore_wait(barrier, F + T - 2)
-            if s < 3:
-                send_maxima(s)
-            elif s == S - 1:
-                send_maxima(3)
-        else:
-            if s < 4:
-                wait_maxima(s)
-            send_stage(s, slot)
-        if v == 3:
-            for copy in norm_inputs():
-                copy.wait()
-            for k in range(K):
-                part = pl.ds(k * LANES, LANES)
-                norm_out[me, tp * K + k] = norm_in[0:1, part] + norm_in[1:2, part]
-
-            @pl.loop(0, F - 1)
-            def _(j):
-                norm_copy(peer(j), me).start()
+    def send_early(begin, end):
+        @pl.loop(begin, end)
+        def _(j):
+            for copy in early_copies(j, cross(j), me):
+                copy.start()
+
+    pl.semaphore_wait(barrier, F + T - 2)
+    send_early(0, 1)
+    visit_maxima(0, 2)
+    send_maxima(0)
+    send_early(1, EARLY)
+    for s in range(1, S):
+        if s == min(AHEAD, S - 1):
+            wait_maxima(0)
+            send_pairs(0, 2, 0, 1)
+        prefetch(s)
+        visit_maxima(s, (s - 1) % 2)
+    send_maxima(1)
+    send_pairs(0, 2, 1, H // 2)
+    wait_maxima(1)
+    reduce_maxima()
+    send_maxima(2)
+    send_pairs(0, 2, H // 2, H - 1)
+    send_last(0, 2)
+
+    for copy in norm_inputs():
+        copy.wait()
+    for k in range(K):
+        part = pl.ds(k * LANES, LANES)
+        norm_out[me, tp * K + k] = norm_in[0:1, part] + norm_in[1:2, part]
+
+    @pl.loop(0, F - 1)
+    def _(j):
+        norm_copy(peer(j), me).start()
+
+    wait_maxima(2)
+    for s in range(1, S):
+        v = S - 2 + s
+        prefetch(v + 1)
+        send_pairs(s, v % 2, 0, H - 1)
+        send_last(s, v % 2)
+        if s == subs - 1:
+            finish_early()
 
     @pl.loop(0, F - 1)
     def _(j):
@@ -270,19 +367,25 @@
     def _(j):
         share(other(j), other(j)).wait()
 
-    for group in range(4):
+    for kind in range(3):
 
         @pl.loop(0, F - 1)
         def _(j):
-            maxima_copy(group, peer(j), me).wait_send()
+            maxima_copy(kind, peer(j), me).wait_send()
 
     for s in range(S):
 
-        @pl.loop(0, F - 1)
+        @pl.loop(0, H)
         def _(j):
             if s >= S - 2:
-                data_copy(s, peer(j), me).wait_send()
-            data_copy(s, peer(j), peer(j)).wait_recv()
+                data_copy(s, cross(j), me).wait_send()
+            on_data(s, source(j), source(j), j, lambda copy: copy.wait_recv())
+
+        @pl.loop(0, H - 1)
+        def _(j):
+            if s >= S - 2:
+                data_copy(s, near(j), me).wait_send()
+            data_copy(s, near(j), near(j)).wait_recv()
 
 
 def entry(F, T, *refs):
@@ -321,6 +424,7 @@
     f32, bf16 = jnp.float32, jnp.bfloat16
     hbm = pl.BlockSpec(memory_space=pl.ANY)
     vmem = pl.BlockSpec(memory_space=pltpu.VMEM)
+    operands = (lq.T, lk.T, lv.T, hq, hk, hv, wq, wk, wv, norm_train, norm_step)
     *ready, factors, norm = pl.pallas_call(
         functools.partial(entry, F, T),
         out_shape=[pltpu.VMEM((F * rows, C), bf16)] * 3
@@ -332,23 +436,29 @@
             pltpu.VMEM((3, rank, width), bf16),
             pltpu.VMEM((3, rows, rank), bf16),
             pltpu.VMEM((2, N), f32),
+            pltpu.VMEM((3, F, rows, LANES), bf16),
             pltpu.VMEM((2, F, rows, LANES), bf16),
-            pltpu.VMEM((2, F, rows, LANES), bf16),
-            pltpu.VMEM((S, F, F, LANES), f32),
+            pltpu.VMEM((F, F, LANES), f32),
+            pltpu.VMEM((F, S, LANES), f32),
+            pltpu.VMEM((F, S, LANES), f32),
+            pltpu.VMEM((F, S, LANES), f32),
             pltpu.SemaphoreType.DMA((3, 2)),
             pltpu.SemaphoreType.DMA((2,)),
-            pltpu.SemaphoreType.DMA((2, F)),
+            pltpu.SemaphoreType.DMA((3, F)),
             pltpu.SemaphoreType.DMA((2, F)),
             pltpu.SemaphoreType.DMA((S, F)),
-            pltpu.SemaphoreType.DMA((4, F)),
-            pltpu.SemaphoreType.DMA((4, F)),
+            pltpu.SemaphoreType.DMA((3, F)),
+            pltpu.SemaphoreType.DMA((3, F)),
+            pltpu.VMEM((EARLY, rank, LANES), bf16),
+            pltpu.SemaphoreType.DMA((EARLY, 2)),
+            pltpu.SemaphoreType.DMA((EARLY, 2)),
             pltpu.SemaphoreType.DMA((F + T,)),
             pltpu.SemaphoreType.DMA((F + T,)),
         ],
         compiler_params=pltpu.CompilerParams(
-            collective_id=0, has_side_effects=True, vmem_limit_bytes=30000000
+            collective_id=0, has_side_effects=True, vmem_limit_bytes=24000000
         ),
-    )(lq.T, lk.T, lv.T, hq, hk, hv, wq, wk, wv, norm_train, norm_step)
+    )(*[pltpu.with_memory_space_constraint(a, pltpu.HBM) for a in operands])
     norm = norm.reshape(F * T * K, 1, LANES)
     results = pl.pallas_call(
         finish_kernel,
@@ -433,7 +543,7 @@
     def step(*args):
         rows, width = args[0].shape
         aligned = width % (F * LANES) == 0 and args[9].shape[0] % LANES == 0
-        if not aligned or width < 2 * F * LANES or rows % 16 or F % 4 or T < 2:
+        if not aligned or width < 2 * F * LANES or rows % LANES or F % 4 or F < 8 or T < 2:
             return local(*args)
         return fused(F, T, *args)
 

time: 647 us -> 631 us (0.975)
  Pallas kernels: 636 us -> 627 us
  local copies, waits for them, and re-layouts: 7.42 us -> 0 us
    pallas_call x1, Pallas kernels: 626 us -> 617 us  [fused(): pl.pallas_call(functools.partial(entry, F, T), out_shape=[pltpu.VMEM((F *...]
    unnamed x4 -> x0, local copies, waits for them, and re-layouts: 7.42 us -> none
where the time goes in v2:
time: 631 us; the launch traced here: 628 us
  Pallas kernels  627 us (99%)
    pallas_call x1, Pallas kernels, fused(): pl.pallas_call(functools.partial(entry, F, T), out_shape=[pltpu.VMEM((F *...  617 us

profile of v2, /device:TPU:14, one launch (start us, length us, event | category | flops | bytes accessed | tf_op | source)
XLA Modules:
  0.0 627.8 jit_solution(9335640143554368920)
XLA Ops:
  0.6 617.3 %shard_map.162 = (bf16[12288,384]{1,0:T(8,128)(2,1)S(1)}, bf16[12288,384]{1,0:T(8,128)(2,1)S(1)}, bf16[12288,384]{1,0:T(8,128)(2,1)S(1)}, f32[9,1,128]{2,1,0:T(1,128)S(1)}, f32[8,12,1,128]{3,2,1,0:T(1,128)S(1)}) custom-call(bf16[64,1536]{1,0:T(8,128)(2,1)} %bitcast.9, bf16[64,1536]{1,0:T(8,128)(2,1)} %bitcast.10, bf16[64,1536]{1,0:T(8,128)(2,1)} %bitcast.11, ...), custom_call_target="tpu_custom_call" | custom-call | tf_op jit(solution)/shard_map/pallas_call | solution.py:428
  617.9 9.8 %shard_map.163 = (bf16[12288,384]{1,0:T(8,128)(2,1)}, bf16[12288,384]{1,0:T(8,128)(2,1)}, bf16[12288,384]{1,0:T(8,128)(2,1)}, f32[3,128]{1,0:T(4,128)}, f32[3,12...) custom-call(bf16[12288,384]{1,0:T(8,128)(2,1)S(1)} %get-tuple-element.19.refs_0_, ...), custom_call_target="tpu_custom_call" | custom-call | tf_op jit(solution)/shard_map/pallas_call | solution.py:463

commit v3 on v2

--- a/solution.py
+++ b/solution.py
@@ -9,8 +9,10 @@
 
 MESH = pl.DeviceIdType.MESH
 LANES = 128
-EARLY = 2
+EARLY = 1
 AHEAD = 3
+CHUNKS = 2
+PARTS = 4
 
 
 def merge_kernel(
@@ -54,6 +56,7 @@
     H = F // 2
     G = H // 2
     R = rows if rows <= 1536 else 768 if rows % 768 == 0 else rows
+    rows_c = rows // CHUNKS
     me = lax.axis_index("fsdp")
     tp = lax.axis_index("tp")
     half, place = me // H, me % H
@@ -109,8 +112,7 @@
     def norm_inputs():
         return [pltpu.make_async_copy(norms[i], norm_in.at[i], norm_sem.at[i]) for i in range(2)]
 
-    def merged(s, slot, t, r):
-        part = pl.ds(pl.multiple_of(r * R, R), R)
+    def merged(s, slot, t, part):
         product = jnp.dot(
             low_s[s // subs, part, :],
             high[s // subs, :, columns(s, t)],
@@ -124,7 +126,7 @@
             load(s, slot, t).wait()
 
             def step(r, most):
-                size = jnp.abs(merged(s, slot, t, r))
+                size = jnp.abs(merged(s, slot, t, pl.ds(pl.multiple_of(r * R, R), R)))
                 return jnp.maximum(most, jnp.max(size.reshape(R // 8, 8, LANES), axis=0))
 
             most = lax.fori_loop(0, rows // R, step, jnp.zeros((8, LANES), f32))
@@ -181,24 +183,52 @@
         return pltpu.make_async_remote_copy(
             src_ref=sbuf.at[s % 2, t, pl.ds(skip, rows - skip)],
             dst_ref=outs[s // subs].at[pl.ds(start, rows - skip), lanes],
-            send_sem=send_sem.at[s % 2, t],
+            send_sem=send_sem.at[s % 2, t, 0],
             recv_sem=recv_sem.at[s, source],
             device_id={"fsdp": t},
             device_id_type=MESH,
         )
 
-    def on_data(s, t, source, j, act):
+    def chunk_copy(s, t, q, early=False):
+        lanes = pl.ds((s % subs) * LANES, LANES)
+        skip = LANES if early else 0
+        begin = pl.multiple_of(q * rows_c + skip, LANES)
+        start = pl.multiple_of(me * rows + q * rows_c + skip, LANES)
+        return pltpu.make_async_remote_copy(
+            src_ref=sbuf.at[s % 2, t, pl.ds(begin, rows_c - skip)],
+            dst_ref=outs[s // subs].at[pl.ds(start, rows_c - skip), lanes],
+            send_sem=send_sem.at[s % 2, t, q],
+            recv_sem=recv_sem.at[s, me],
+            device_id={"fsdp": t},
+            device_id_type=MESH,
+        )
+
+    def on_chunk(s, t, q, j, act):
         if s >= subs or j is None:
-            act(data_copy(s, t, source))
+            act(chunk_copy(s, t, q))
+        else:
+            short = (j < EARLY) & (q == 0)
+
+            @pl.when(short)
+            def _():
+                act(chunk_copy(s, t, q, True))
+
+            @pl.when(jnp.logical_not(short))
+            def _():
+                act(chunk_copy(s, t, q))
+
+    def wait_data(s, source, j):
+        if s >= subs or j is None:
+            data_copy(s, source, source).wait_recv()
         else:
 
             @pl.when(j < EARLY)
             def _():
-                act(data_copy(s, t, source, True))
+                data_copy(s, source, source, True).wait_recv()
 
             @pl.when(j >= EARLY)
             def _():
-                act(data_copy(s, t, source))
+                data_copy(s, source, source).wait_recv()
 
     def early_copies(j, t, source):
         piece = pl.ds(0, LANES)
@@ -232,39 +262,42 @@
                 value = outs[0][part, lanes].astype(f32) + product
                 outs[0][part, lanes] = (value * (1.0 / factor(s, me))).astype(jnp.bfloat16)
 
-    def scaled(s, slot, t, put):
+    def send_chunk(s, slot, t, q, j=None):
         if s > 0:
-            load(s, slot, t).wait()
-        inverse = 1.0 / factor(s, t)
+
+            @pl.when(q == 0)
+            def _():
+                load(s, slot, t).wait()
+
+        if s >= 2:
+            on_chunk(s - 2, t, q, j, lambda copy: copy.wait_send())
+        part = pl.ds(pl.multiple_of(q * rows_c, LANES), rows_c)
+        value = merged(s, slot, t, part) * (1.0 / factor(s, t))
+        sbuf[s % 2, t, part, :] = value.astype(jnp.bfloat16)
+        on_chunk(s, t, q, j, lambda copy: copy.start())
+
+    def send_pairs(s, slot, begin, end):
+        @pl.loop(0, CHUNKS)
+        def _(q):
+            @pl.loop(begin, end)
+            def _(j):
+                send_chunk(s, slot, cross(j), q, j)
+
+                @pl.when(j < H - 1)
+                def _():
+                    send_chunk(s, slot, near(j % (H - 1)), q)
+
+    def keep_own(s, slot):
+        if s > 0:
+            load(s, slot, me).wait()
+        inverse = 1.0 / factor(s, me)
+        lanes = pl.ds((s % subs) * LANES, LANES)
 
         @pl.loop(0, rows // R)
         def _(r):
-            put(r, (merged(s, slot, t, r) * inverse).astype(jnp.bfloat16))
-
-    def send_block(s, slot, t, j=None):
-        if s >= 2:
-            on_data(s - 2, t, me, j, lambda copy: copy.wait_send())
-
-        def put(r, value):
-            sbuf[s % 2, t, pl.ds(pl.multiple_of(r * R, R), R), :] = value
-
-        scaled(s, slot, t, put)
-        on_data(s, t, me, j, lambda copy: copy.start())
-
-    def send_pairs(s, slot, begin, end):
-        @pl.loop(begin, end)
-        def _(j):
-            send_block(s, slot, cross(j), j)
-            send_block(s, slot, near(j))
-
-    def send_last(s, slot):
-        send_block(s, slot, cross(H - 1), H - 1)
-
-        def put(r, value):
-            lanes = pl.ds((s % subs) * LANES, LANES)
-            outs[s // subs][pl.ds(pl.multiple_of(me * rows + r * R, R), R), lanes] = value
-
-        scaled(s, slot, me, put)
+            value = merged(s, slot, me, pl.ds(pl.multiple_of(r * R, R), R)) * inverse
+            part = pl.ds(pl.multiple_of(me * rows + r * R, R), R)
+            outs[s // subs][part, lanes] = value.astype(jnp.bfloat16)
 
     queue = [(kind, s) for kind in (1, 2) for s in range(1, S)]
 
@@ -307,11 +340,10 @@
             for copy in early_copies(j, cross(j), me):
                 copy.start()
 
+    visit_maxima(0, 2)
     pl.semaphore_wait(barrier, F + T - 2)
-    send_early(0, 1)
-    visit_maxima(0, 2)
     send_maxima(0)
-    send_early(1, EARLY)
+    send_early(0, EARLY)
     for s in range(1, S):
         if s == min(AHEAD, S - 1):
             wait_maxima(0)
@@ -323,8 +355,8 @@
     wait_maxima(1)
     reduce_maxima()
     send_maxima(2)
-    send_pairs(0, 2, H // 2, H - 1)
-    send_last(0, 2)
+    send_pairs(0, 2, H // 2, H)
+    keep_own(0, 2)
 
     for copy in norm_inputs():
         copy.wait()
@@ -340,8 +372,8 @@
     for s in range(1, S):
         v = S - 2 + s
         prefetch(v + 1)
-        send_pairs(s, v % 2, 0, H - 1)
-        send_last(s, v % 2)
+        send_pairs(s, v % 2, 0, H)
+        keep_own(s, v % 2)
         if s == subs - 1:
             finish_early()
 
@@ -374,18 +406,21 @@
             maxima_copy(kind, peer(j), me).wait_send()
 
     for s in range(S):
+        if s >= S - 2:
+
+            @pl.loop(0, F - 1)
+            def _(j):
+                @pl.loop(0, CHUNKS)
+                def _(q):
+                    chunk_copy(s, peer(j), q).wait_send()
 
         @pl.loop(0, H)
         def _(j):
-            if s >= S - 2:
-                data_copy(s, cross(j), me).wait_send()
-            on_data(s, source(j), source(j), j, lambda copy: copy.wait_recv())
+            wait_data(s, source(j), j)
 
         @pl.loop(0, H - 1)
         def _(j):
-            if s >= S - 2:
-                data_copy(s, near(j), me).wait_send()
-            data_copy(s, near(j), near(j)).wait_recv()
+            wait_data(s, near(j), None)
 
 
 def entry(F, T, *refs):
@@ -396,8 +431,15 @@
 def finish_kernel(*refs):
     ready, (factors, norm), ready_out, factor_out = refs[0:3], refs[3:5], refs[5:8], refs[8:11]
     norm_out, factor_buf, norm_buf, ready_sem, small_sem = refs[11:]
+    part = ready[0].shape[0] // PARTS
     copies = [
-        pltpu.make_async_copy(ready[m], ready_out[m], ready_sem.at[m]) for m in range(3)
+        pltpu.make_async_copy(
+            ready[m].at[pl.ds(p * part, part)],
+            ready_out[m].at[pl.ds(p * part, part)],
+            ready_sem.at[m, p],
+        )
+        for p in range(PARTS)
+        for m in range(3)
     ]
     subs = factors.shape[0] // 3
     for copy in copies:
@@ -445,7 +487,7 @@
             pltpu.SemaphoreType.DMA((3, 2)),
             pltpu.SemaphoreType.DMA((2,)),
             pltpu.SemaphoreType.DMA((3, F)),
-            pltpu.SemaphoreType.DMA((2, F)),
+            pltpu.SemaphoreType.DMA((2, F, CHUNKS)),
             pltpu.SemaphoreType.DMA((S, F)),
             pltpu.SemaphoreType.DMA((3, F)),
             pltpu.SemaphoreType.DMA((3, F)),
@@ -470,7 +512,7 @@
         scratch_shapes=[
             pltpu.VMEM((3, subs, LANES), f32),
             pltpu.VMEM((F * T * K, LANES), bf16),
-            pltpu.SemaphoreType.DMA((3,)),
+            pltpu.SemaphoreType.DMA((3, PARTS)),
             pltpu.SemaphoreType.DMA((4,)),
         ],
         compiler_params=pltpu.CompilerParams(vmem_limit_bytes=2000000),
@@ -543,7 +585,7 @@
     def step(*args):
         rows, width = args[0].shape
         aligned = width % (F * LANES) == 0 and args[9].shape[0] % LANES == 0
-        if not aligned or width < 2 * F * LANES or rows % LANES or F % 4 or F < 8 or T < 2:
+        if not aligned or width < 2 * F * LANES or rows % (CHUNKS * LANES) or F % 4 or F < 8 or T < 2:
             return local(*args)
         return fused(F, T, *args)
 

time: 631 us -> 630 us (level)
  no operation moved by 1% of the time
where the time goes in v3:
time: 630 us; the launch traced here: 628 us
  Pallas kernels  628 us (100%)
    pallas_call x1, Pallas kernels, fused(): pl.pallas_call(functools.partial(entry, F, T), out_shape=[pltpu.VMEM((F *...  618 us

profile of v3, /device:TPU:14, one launch (start us, length us, event | category | flops | bytes accessed | tf_op | source)
XLA Modules:
  0.0 628.3 jit_solution(9792733968606848795)
XLA Ops:
  0.6 618.2 %shard_map.162 = (bf16[12288,384]{1,0:T(8,128)(2,1)S(1)}, bf16[12288,384]{1,0:T(8,128)(2,1)S(1)}, bf16[12288,384]{1,0:T(8,128)(2,1)S(1)}, f32[9,1,128]{2,1,0:T(1,128)S(1)}, f32[8,12,1,128]{3,2,1,0:T(1,128)S(1)}) custom-call(bf16[64,1536]{1,0:T(8,128)(2,1)} %bitcast.9, bf16[64,1536]{1,0:T(8,128)(2,1)} %bitcast.10, bf16[64,1536]{1,0:T(8,128)(2,1)} %bitcast.11, ...), custom_call_target="tpu_custom_call" | custom-call | tf_op jit(solution)/shard_map/pallas_call | solution.py:470
  618.8 9.5 %shard_map.163 = (bf16[12288,384]{1,0:T(8,128)(2,1)}, bf16[12288,384]{1,0:T(8,128)(2,1)}, bf16[12288,384]{1,0:T(8,128)(2,1)}, f32[3,128]{1,0:T(4,128)}, f32[3,12...) custom-call(bf16[12288,384]{1,0:T(8,128)(2,1)S(1)} %get-tuple-element.19.refs_0_, ...), custom_call_target="tpu_custom_call" | custom-call | tf_op jit(solution)/shard_map/pallas_call | solution.py:505
